TPU v7x, 32 devices: a whole 2x2x4 slice. The times are simulated.
32 devices in a mesh: mesh: 4 (over y, x), sub: 8 (over z, core).
Axes of the slice: x: 2, y: 2, z: 4, core: 2. Of those that a mesh axis runs over, the one named last changes fastest.
Arguments:
- displacement: float32 [3, 2, 32, 1024], P(None, None, 'mesh', 'sub'), may hold values from -4 to 4
- velocity: float32 [3, 2, 32, 1024], P(None, None, 'mesh', 'sub'), may hold values from -6 to 6
- node_mass: float32 [2, 32, 1024], P(None, 'mesh', 'sub'), may hold values from 0.5 to 2
- moduli: float32 [2, 32, 1024], P(None, 'mesh', 'sub'), may hold values from 0.5 to 2
- stiffness: float32 [24, 24], replicated, may hold values from -0.45 to 12, as said below
- surface_ref: float32 [3, 32, 1024], P(None, 'mesh', 'sub'), may hold values from -6 to 6
- facets: float32 [4, 8, 6, 1024], P('mesh', 'sub'), may hold values from -6 to 6
- penalty: float32 [4, 8, 1024], P('mesh', 'sub'), may hold values from 0.5 to 4
- owners: int32 [2, 4, 8, 8, 1], P(None, 'mesh', 'sub'), may hold values from 0 to 3; in each aligned block of 8 rows (0 to 7, 8 to 15, ..., all dimensions but the last counted through in order) at most 4 rows name the same one
- facet_pairs: int32 [2, 32, 1024], P(None, 'mesh', 'sub'), may hold values from 0 to 1023
Outputs:
- final_displacement: float32 [3, 2, 32, 1024], P(None, None, 'mesh', 'sub')
- final_velocity: float32 [3, 2, 32, 1024], P(None, None, 'mesh', 'sub')
Inputs may be any that keep to these rules, and one draw needn't show every extreme that they name: `owners`: in every step no device sends more than 4 of its blocks to one owner, and some device sends exactly 4 to one owner. `stiffness`: Symmetric.
All inputs are finite; a program needn't handle non-finite values.
Results may differ from a plain program's by a relative error of at most 0.0001.
Values sent between devices are 32-bit elements; how exact they have to be, the bound alone decides.
A program may use at most 64 MiB of HBM per device.

v0:
```python
import jax
import jax.numpy as jnp
from jax import lax
from jax.sharding import PartitionSpec as P

TIME_STEP = 0.1
CORNER_SHIFTS = (
    (0, 0, 0),
    (0, 0, 1),
    (0, 1, 0),
    (0, 1, 1),
    (1, 0, 0),
    (1, 0, 1),
    (1, 1, 0),
    (1, 1, 1),
)


def with_halo(shard, sides, width):
    for axis, dim in sides:
        size, length = (lax.axis_size(axis), shard.shape[dim])
        up = [(i, (i + 1) % size) for i in range(size)]
        down = [(j, i) for i, j in up]
        last = lax.slice_in_dim(shard, length - width, length, axis=dim)
        leading = lax.slice_in_dim(shard, 0, width, axis=dim)
        before = lax.ppermute(last, axis, up)
        after = lax.ppermute(leading, axis, down)
        shard = jnp.concatenate([before, shard, after], axis=dim)
    return shard


def node_forces(node_patch, patch_moduli, stiffness):
    layers = node_patch.shape[1]
    row_count = node_patch.shape[2] - 2
    col_count = node_patch.shape[3] - 2
    element_scale = jnp.zeros((layers - 1, row_count + 1, col_count + 1), jnp.float32)
    corners = []
    for shift_z, shift_x, shift_y in CORNER_SHIFTS:
        element_scale = (
            element_scale
            + patch_moduli[
                shift_z : shift_z + layers - 1,
                shift_x : shift_x + row_count + 1,
                shift_y : shift_y + col_count + 1,
            ]
        )
        corners.append(
            node_patch[
                :,
                shift_z : shift_z + layers - 1,
                shift_x : shift_x + row_count + 1,
                shift_y : shift_y + col_count + 1,
            ]
        )
    element_scale = element_scale * 0.125
    stacked = jnp.concatenate(corners, axis=0).reshape(24, -1)
    forces = (
        jnp.dot(stiffness, stacked, precision=lax.Precision.HIGHEST).reshape(
            24, layers - 1, row_count + 1, col_count + 1
        )
        * element_scale[None]
    )
    summed = jnp.zeros((3, layers, row_count, col_count), jnp.float32)
    for corner, (shift_z, shift_x, shift_y) in enumerate(CORNER_SHIFTS):
        contribution = forces[
            3 * corner : 3 * corner + 3,
            :,
            1 - shift_x : 1 - shift_x + row_count,
            1 - shift_y : 1 - shift_y + col_count,
        ]
        summed = summed.at[:, shift_z : shift_z + layers - 1].add(contribution)
    return summed


def contact_push(points, facet_rows, stiffness_row):
    normal_gap = jnp.sum(facet_rows[3:6] * (points - facet_rows[0:3]), axis=0)
    return facet_rows[3:6] * (stiffness_row * jnp.maximum(-normal_gap, 0.0))[None]


def shards(
    displacement,
    velocity,
    node_mass,
    moduli,
    stiffness,
    surface_ref,
    facets,
    penalty,
    owners,
    facet_pairs,
):
    steps = owners.shape[0]
    row_count = displacement.shape[2]
    col_count = displacement.shape[3]
    table_width = facets.shape[3]
    ext_moduli = with_halo(moduli, (("mesh", 1), ("sub", 2)), 1)
    every_table, every_stiff = (
        lax.all_gather(facets, "mesh", axis=0, tiled=True),
        lax.all_gather(penalty, "mesh", axis=0, tiled=True),
    )
    wide_table = every_table[:, 0].transpose(1, 0, 2).reshape(6, -1)
    wide_stiff = every_stiff[:, 0].reshape(-1)
    for step_index in range(steps):
        node_patch = with_halo(displacement, (("mesh", 2), ("sub", 3)), 1)
        internal = node_forces(node_patch, ext_moduli, stiffness)
        points = surface_ref + displacement[:, 0]
        pair_rows = facet_pairs[step_index]
        destination = owners[step_index, 0, 0, :, 0]
        lookup = (destination[:, None] * table_width + pair_rows).reshape(-1)
        facet_rows = jnp.take(wide_table, lookup, axis=1)
        pushed = contact_push(points.reshape(3, -1), facet_rows, jnp.take(wide_stiff, lookup))
        surface_push = pushed.reshape(3, row_count, col_count)
        net_force = (-internal).at[:, 0].add(surface_push)
        velocity = velocity + TIME_STEP * net_force / node_mass[None]
        displacement = displacement + TIME_STEP * velocity
    return (displacement, velocity)


def solution(mesh):
    in_specs = (
        P(None, None, "mesh", "sub"),
        P(None, None, "mesh", "sub"),
        P(None, "mesh", "sub"),
        P(None, "mesh", "sub"),
        P(),
        P(None, "mesh", "sub"),
        P("mesh", "sub", None, None),
        P("mesh", "sub", None),
        P(None, "mesh", "sub", None, None),
        P(None, "mesh", "sub"),
    )
    out_specs = (P(None, None, "mesh", "sub"), P(None, None, "mesh", "sub"))
    return jax.shard_map(shards, mesh=mesh, in_specs=in_specs, out_specs=out_specs, check_vma=False)
```

profile of v0, /device:TPU:0, one launch (start us, length us, event | category | flops | bytes accessed | tf_op | source)
XLA Modules:
  0.0 73.5 jit_solution(7916683548548712662)
XLA Ops:
  0.7 0.8 %fusion.23 = (f32[3,2,1,128]{3,2,1,0:T(1,128)S(1)}, f32[3,2,1,128]{3,2,1,0:T(1,128)S(1)}) fusion(f32[3,2,8,128]{3,2,1,0:T(8,128)} %param.50), kind=kLoop, calls=%fused_computation.108 | loop fusion | bytes 12288 | tf_op jit(solution)/shard_map/slice | solution.py:24
  1.5 3.0 %collective-permute-start = (f32[3,2,1,128]{3,2,1,0:T(1,128)S(1)}, f32[3,2,1,128]{3,2,1,0:T(1,128)S(1)}, u32[]{:S(2)}, u32[]{:S(2)}) collective-permute-start(f32[3,2,1,128]{3,2,1,0:T(1,128)S(1)} %get-tuple-element.236), channel_id=1, source_target_pairs={{0,8},{8,16},{16,24},{24,0},{1,9},{9,17},{17,25},{25,1},{2,10},{10... | collective-permute-start | bytes 9224 | tf_op jit(solution)/shard_map/ppermute | solution.py:26
  4.5 1.0 %collective-permute-start.1 = (f32[3,2,1,128]{3,2,1,0:T(1,128)S(1)}, f32[3,2,1,128]{3,2,1,0:T(1,128)S(1)}, u32[]{:S(2)}, u32[]{:S(2)}) collective-permute-start(f32[3,2,1,128]{3,2,1,0:T(1,128)S(1)} %get-tuple-element.237), channel_id=1, source_target_pairs={{8,0},{16,8},{24,16},{0,24},{9,1},{17,9},{25,17},{1,25},{10,2},{18... | collective-permute-start | bytes 9224 | tf_op jit(solution)/shard_map/ppermute | solution.py:27
  5.5 0.8 %fusion.25 = (f32[2,1,128]{2,1,0:T(1,128)S(1)}, f32[2,1,128]{2,1,0:T(1,128)S(1)}) fusion(f32[2,8,128]{2,1,0:T(8,128)} %param.53), kind=kLoop, calls=%fused_computation.110 | loop fusion | bytes 4096 | tf_op jit(solution)/shard_map/slice | solution.py:24
  6.3 1.0 %collective-permute-start.4 = (f32[2,1,128]{2,1,0:T(1,128)S(1)}, f32[2,1,128]{2,1,0:T(1,128)S(1)}, u32[]{:S(2)}, u32[]{:S(2)}) collective-permute-start(f32[2,1,128]{2,1,0:T(1,128)S(1)} %get-tuple-element.246), channel_id=1, source_target_pairs={{0,8},{8,16},{16,24},{24,0},{1,9},{9,17},{17,25},{25,1},{2,10},{10... | collective-permute-start | bytes 3080 | tf_op jit(solution)/shard_map/ppermute | solution.py:26
  7.3 1.9 %collective-permute-start.5 = (f32[2,1,128]{2,1,0:T(1,128)S(1)}, f32[2,1,128]{2,1,0:T(1,128)S(1)}, u32[]{:S(2)}, u32[]{:S(2)}) collective-permute-start(f32[2,1,128]{2,1,0:T(1,128)S(1)} %get-tuple-element.247), channel_id=1, source_target_pairs={{8,0},{16,8},{24,16},{0,24},{9,1},{17,9},{25,17},{1,25},{10,2},{18... | collective-permute-start | bytes 3080 | tf_op jit(solution)/shard_map/ppermute | solution.py:27
  9.2 0.7 multiply_bitcast_fusion
  9.9 0.8 %fusion.19 = (s32[1024]{0:T(1024)S(1)}, s32[1024]{0:T(1024)S(1)}) fusion(s32[2,8,128]{2,1,0:T(8,128)} %param.59, s32[8]{0:T(128)S(1)} %get-tuple-element.248, s32[8]{0:T(128)S(1)} %get-tuple-element.249), kind=kLoop, calls=%fused_computation.102 | loop fusion | flops 10240 | bytes 16448 | tf_op gather
  10.6 0.8 %compare_and_fusion = (pred[1024]{0:T(1024)(128)(4,1)S(1)}, pred[1024]{0:T(1024)(128)(4,1)S(1)}) fusion(s32[2,8,128]{2,1,0:T(8,128)} %param.59, s32[8]{0:T(128)S(1)} %get-tuple-element.248, s32[8]{0:T(128)S(1)} %get-tuple-element.249), kind=kLoop, calls=%fused_computation.99 | loop fusion | flops 14336 | bytes 10304 | tf_op jit(solution)/shard_map/jit(_take)/and | solution.py:110
  11.4 8.8 %all_gather.6 = f32[4,1,6,1024]{3,1,2,0:T(1,128)S(1)} all-gather(f32[1,1,6,1024]{3,1,2,0:T(1,128)} %param.56), channel_id=1, replica_groups=mesh['mesh'=4,'sub'=8] {'mesh'}, dimensions={0}, use_global_device_ids=true | all-gather | bytes 122880 | tf_op jit(solution)/shard_map/all_gather | solution.py:98
  20.2 0.7 copy.32
  20.9 2.8 %gather_fusion = f32[1024,6]{1,0:T(8,128)S(1)} fusion(f32[6,4096]{0,1:T(8,128)S(1)} %bitcast.71, s32[1024]{0:T(1024)S(1)} %get-tuple-element.245), kind=kCustom, calls=%fused_computation.clone | custom fusion | bytes 53248 | tf_op jit(solution)/shard_map/jit(_take)/gather | solution.py:110
  23.7 2.8 %gather_fusion.2 = f32[1024,6]{1,0:T(8,128)S(1)} fusion(f32[6,4096]{0,1:T(8,128)S(1)} %bitcast.72, s32[1024]{0:T(1024)S(1)} %get-tuple-element.244), kind=kCustom, calls=%fused_computation.2.clone | custom fusion | bytes 53248 | tf_op jit(solution)/shard_map/jit(_take)/gather | solution.py:110
  26.8 7.5 %all_gather.7 = f32[4,1,1024]{2,1,0:T(1,128)S(1)} all-gather(f32[1,1,1024]{2,1,0:T(1,128)S(1)} %copy-done.6), channel_id=1, replica_groups=mesh['mesh'=4,'sub'=8] {'mesh'}, dimensions={0}, use_global_device_ids=true | all-gather | bytes 20480 | tf_op jit(solution)/shard_map/all_gather | solution.py:99
  34.3 6.1 %gather_fusion.1 = f32[1024]{0:T(1024)S(1)} fusion(f32[4096]{0:T(1024)S(1)} %bitcast.69, s32[1024]{0:T(1024)S(1)} %get-tuple-element.245), kind=kCustom, calls=%fused_computation.1.clone | custom fusion | bytes 12288 | tf_op jit(solution)/shard_map/jit(_take)/gather | solution.py:111
  40.5 0.3 select_bitcast_fusion
  40.8 0.4 fusion.3
  41.2 0.3 slice_multiply_fusion.1
  41.6 6.2 %gather_fusion.3 = f32[1024]{0:T(1024)S(1)} fusion(f32[4096]{0:T(1024)S(1)} %bitcast.70, s32[1024]{0:T(1024)S(1)} %get-tuple-element.244), kind=kCustom, calls=%fused_computation.3.clone | custom fusion | bytes 12288 | tf_op jit(solution)/shard_map/jit(_take)/gather | solution.py:111
  48.0 3.5 %collective-permute-start.7 = (f32[2,10,1]{2,1,0:T(8,128)S(1)}, f32[2,10,1]{2,1,0:T(8,128)S(1)}, u32[]{:S(2)}, u32[]{:S(2)}) collective-permute-start(f32[2,10,1]{2,1,0:T(8,128)S(1)} %get-tuple-element.239), channel_id=1, source_target_pairs={{1,0},{2,1},{3,2},{4,3},{5,4},{6,5},{7,6},{0,7},{9,8},{10,9},{11,1... | collective-permute-start | bytes 248 | tf_op jit(solution)/shard_map/ppermute | solution.py:27
  51.6 1.4 %collective-permute-done.6 = f32[2,10,1]{2,1,0:T(8,128)S(1)} collective-permute-done((f32[2,10,1]{2,1,0:T(8,128)S(1)}, f32[2,10,1]{2,1,0:T(8,128)S(1)}, u32[]{:S(2)}, u32[]{:S(2)}) %collective-permute-start.6) | collective-permute-done | bytes 112 | tf_op jit(solution)/shard_map/ppermute | solution.py:26
  53.3 3.5 %collective-permute-start.3 = (f32[3,2,10,1]{3,2,1,0:T(8,128)S(1)}, f32[3,2,10,1]{3,2,1,0:T(8,128)S(1)}, u32[]{:S(2)}, u32[]{:S(2)}) collective-permute-start(f32[3,2,10,1]{3,2,1,0:T(8,128)S(1)} %get-tuple-element.228), channel_id=1, source_target_pairs={{1,0},{2,1},{3,2},{4,3},{5,4},{6,5},{7,6},{0,7},{9,8},{10,9},{11,1... | collective-permute-start | bytes 728 | tf_op jit(solution)/shard_map/ppermute | solution.py:27
  56.8 1.7 %collective-permute-done.2 = f32[3,2,10,1]{3,2,1,0:T(8,128)S(1)} collective-permute-done((f32[3,2,10,1]{3,2,1,0:T(8,128)S(1)}, f32[3,2,10,1]{3,2,1,0:T(8,128)S(1)}, u32[]{:S(2)}, u32[]{:S(2)}) %collective-permute-start.2) | collective-permute-done | bytes 272 | tf_op jit(solution)/shard_map/ppermute | solution.py:26
  60.4 1.3 %collective-permute-start.8 = (f32[3,2,1,128]{3,2,0,1:T(1,128)S(1)}, f32[3,2,1,128]{3,2,0,1:T(1,128)S(1)}, u32[]{:S(2)}, u32[]{:S(2)}) collective-permute-start(f32[3,2,1,128]{3,2,0,1:T(1,128)S(1)} %get-tuple-element.234), channel_id=1, source_target_pairs={{0,8},{8,16},{16,24},{24,0},{1,9},{9,17},{17,25},{25,1},{2,10},{10... | collective-permute-start | bytes 9224 | tf_op jit(solution)/shard_map/ppermute | solution.py:26
  61.7 1.7 %collective-permute-start.9 = (f32[3,2,1,128]{3,2,0,1:T(1,128)S(1)}, f32[3,2,1,128]{3,2,0,1:T(1,128)S(1)}, u32[]{:S(2)}, u32[]{:S(2)}) collective-permute-start(f32[3,2,1,128]{3,2,0,1:T(1,128)S(1)} %get-tuple-element.235), channel_id=1, source_target_pairs={{8,0},{16,8},{24,16},{0,24},{9,1},{17,9},{25,17},{1,25},{10,2},{18... | collective-permute-start | bytes 9224 | tf_op jit(solution)/shard_map/ppermute | solution.py:27
  63.4 0.4 fusion.1
  63.8 1.2 %collective-permute-done.8 = f32[3,2,1,128]{3,2,0,1:T(1,128)S(1)} collective-permute-done((f32[3,2,1,128]{3,2,0,1:T(1,128)S(1)}, f32[3,2,1,128]{3,2,0,1:T(1,128)S(1)}, u32[]{:S(2)}, u32[]{:S(2)}) %collective-permute-start.8) | collective-permute-done | bytes 3104 | tf_op jit(solution)/shard_map/ppermute | solution.py:26
  65.4 3.5 %collective-permute-start.11 = (f32[3,2,10,1]{3,2,0,1:T(8,128)S(1)}, f32[3,2,10,1]{3,2,0,1:T(8,128)S(1)}, u32[]{:S(2)}, u32[]{:S(2)}) collective-permute-start(f32[3,2,10,1]{3,2,0,1:T(8,128)S(1)} %get-tuple-element.226), channel_id=1, source_target_pairs={{1,0},{2,1},{3,2},{4,3},{5,4},{6,5},{7,6},{0,7},{9,8},{10,9},{11,1... | collective-permute-start | bytes 728 | tf_op jit(solution)/shard_map/ppermute | solution.py:27
  68.9 0.3 slice_multiply_fusion
  69.4 1.2 %collective-permute-done.10 = f32[3,2,10,1]{3,2,0,1:T(8,128)S(1)} collective-permute-done((f32[3,2,10,1]{3,2,0,1:T(8,128)S(1)}, f32[3,2,10,1]{3,2,0,1:T(8,128)S(1)}, u32[]{:S(2)}, u32[]{:S(2)}) %collective-permute-start.10) | collective-permute-done | bytes 272 | tf_op jit(solution)/shard_map/ppermute | solution.py:26
  72.3 0.6 copy.40
  72.9 0.6 copy.41
  (95 shorter events, 4.7 us)
Async XLA Ops:
  0.6 58.3 %copy-start = (f32[24,24]{1,0:T(8,128)S(1)}, f32[24,24]{1,0:T(8,128)}, u32[]{:S(2)}) copy-start(f32[24,24]{1,0:T(8,128)} %param.54) | copy-start | bytes 6916
  0.6 25.9 %copy-start.1 = (f32[3,2,8,128]{3,2,1,0:T(8,128)S(1)}, f32[3,2,8,128]{3,2,1,0:T(8,128)}, u32[]{:S(2)}) copy-start(f32[3,2,8,128]{3,2,1,0:T(8,128)} %param.50) | copy-start | bytes 73732
  0.7 25.9 %copy-start.3 = (f32[3,8,128]{2,1,0:T(8,128)S(1)}, f32[3,8,128]{2,1,0:T(8,128)}, u32[]{:S(2)}) copy-start(f32[3,8,128]{2,1,0:T(8,128)} %param.55) | copy-start | bytes 36868
  0.7 26.1 %copy-start.6 = (f32[1,1,1024]{2,1,0:T(1,128)S(1)}, f32[1,1,1024]{2,1,0:T(1,128)}, u32[]{:S(2)}) copy-start(f32[1,1,1024]{2,1,0:T(1,128)} %param.57) | copy-start | bytes 12292
  1.5 51.6 %collective-permute-start = (f32[3,2,1,128]{3,2,1,0:T(1,128)S(1)}, f32[3,2,1,128]{3,2,1,0:T(1,128)S(1)}, u32[]{:S(2)}, u32[]{:S(2)}) collective-permute-start(f32[3,2,1,128]{3,2,1,0:T(1,128)S(1)} %get-tuple-element.236), channel_id=1, source_target_pairs={{0,8},{8,16},{16,24},{24,0},{1,9},{9,17},{17,25},{25,1},{2,10},{10... | collective-permute-start | bytes 9224 | tf_op jit(solution)/shard_map/ppermute | solution.py:26
  4.5 48.7 %collective-permute-start.1 = (f32[3,2,1,128]{3,2,1,0:T(1,128)S(1)}, f32[3,2,1,128]{3,2,1,0:T(1,128)S(1)}, u32[]{:S(2)}, u32[]{:S(2)}) collective-permute-start(f32[3,2,1,128]{3,2,1,0:T(1,128)S(1)} %get-tuple-element.237), channel_id=1, source_target_pairs={{8,0},{16,8},{24,16},{0,24},{9,1},{17,9},{25,17},{1,25},{10,2},{18... | collective-permute-start | bytes 9224 | tf_op jit(solution)/shard_map/ppermute | solution.py:27
  6.3 41.6 %collective-permute-start.4 = (f32[2,1,128]{2,1,0:T(1,128)S(1)}, f32[2,1,128]{2,1,0:T(1,128)S(1)}, u32[]{:S(2)}, u32[]{:S(2)}) collective-permute-start(f32[2,1,128]{2,1,0:T(1,128)S(1)} %get-tuple-element.246), channel_id=1, source_target_pairs={{0,8},{8,16},{16,24},{24,0},{1,9},{9,17},{17,25},{25,1},{2,10},{10... | collective-permute-start | bytes 3080 | tf_op jit(solution)/shard_map/ppermute | solution.py:26
  7.3 40.6 %collective-permute-start.5 = (f32[2,1,128]{2,1,0:T(1,128)S(1)}, f32[2,1,128]{2,1,0:T(1,128)S(1)}, u32[]{:S(2)}, u32[]{:S(2)}) collective-permute-start(f32[2,1,128]{2,1,0:T(1,128)S(1)} %get-tuple-element.247), channel_id=1, source_target_pairs={{8,0},{16,8},{24,16},{0,24},{9,1},{17,9},{25,17},{1,25},{10,2},{18... | collective-permute-start | bytes 3080 | tf_op jit(solution)/shard_map/ppermute | solution.py:27
  41.5 6.4 %copy-start.4 = (f32[2,8,128]{2,1,0:T(8,128)S(1)}, f32[2,8,128]{2,1,0:T(8,128)}, u32[]{:S(2)}) copy-start(f32[2,8,128]{2,1,0:T(8,128)} %param.53) | copy-start | bytes 24580
  48.0 5.0 %collective-permute-start.6 = (f32[2,10,1]{2,1,0:T(8,128)S(1)}, f32[2,10,1]{2,1,0:T(8,128)S(1)}, u32[]{:S(2)}, u32[]{:S(2)}) collective-permute-start(f32[2,10,1]{2,1,0:T(8,128)S(1)} %get-tuple-element.238), channel_id=1, source_target_pairs={{0,1},{1,2},{2,3},{3,4},{4,5},{5,6},{6,7},{7,0},{8,9},{9,10},{10,1... | collective-permute-start | bytes 248 | tf_op jit(solution)/shard_map/ppermute | solution.py:26
  48.0 5.0 %collective-permute-start.7 = (f32[2,10,1]{2,1,0:T(8,128)S(1)}, f32[2,10,1]{2,1,0:T(8,128)S(1)}, u32[]{:S(2)}, u32[]{:S(2)}) collective-permute-start(f32[2,10,1]{2,1,0:T(8,128)S(1)} %get-tuple-element.239), channel_id=1, source_target_pairs={{1,0},{2,1},{3,2},{4,3},{5,4},{6,5},{7,6},{0,7},{9,8},{10,9},{11,1... | collective-permute-start | bytes 248 | tf_op jit(solution)/shard_map/ppermute | solution.py:27
  53.1 7.0 %copy-start.2 = (f32[3,2,8,128]{3,2,1,0:T(8,128)S(1)}, f32[3,2,8,128]{3,2,1,0:T(8,128)}, u32[]{:S(2)}) copy-start(f32[3,2,8,128]{3,2,1,0:T(8,128)} %param.51) | copy-start | bytes 73732
  53.1 7.0 %copy-start.5 = (f32[2,8,128]{2,1,0:T(8,128)S(1)}, f32[2,8,128]{2,1,0:T(8,128)}, u32[]{:S(2)}) copy-start(f32[2,8,128]{2,1,0:T(8,128)} %param.52) | copy-start | bytes 24580
  53.2 5.3 %collective-permute-start.2 = (f32[3,2,10,1]{3,2,1,0:T(8,128)S(1)}, f32[3,2,10,1]{3,2,1,0:T(8,128)S(1)}, u32[]{:S(2)}, u32[]{:S(2)}) collective-permute-start(f32[3,2,10,1]{3,2,1,0:T(8,128)S(1)} %get-tuple-element.229), channel_id=1, source_target_pairs={{0,1},{1,2},{2,3},{3,4},{4,5},{5,6},{6,7},{7,0},{8,9},{9,10},{10,1... | collective-permute-start | bytes 728 | tf_op jit(solution)/shard_map/ppermute | solution.py:26
  53.3 5.2 %collective-permute-start.3 = (f32[3,2,10,1]{3,2,1,0:T(8,128)S(1)}, f32[3,2,10,1]{3,2,1,0:T(8,128)S(1)}, u32[]{:S(2)}, u32[]{:S(2)}) collective-permute-start(f32[3,2,10,1]{3,2,1,0:T(8,128)S(1)} %get-tuple-element.228), channel_id=1, source_target_pairs={{1,0},{2,1},{3,2},{4,3},{5,4},{6,5},{7,6},{0,7},{9,8},{10,9},{11,1... | collective-permute-start | bytes 728 | tf_op jit(solution)/shard_map/ppermute | solution.py:27
  60.4 4.5 %collective-permute-start.8 = (f32[3,2,1,128]{3,2,0,1:T(1,128)S(1)}, f32[3,2,1,128]{3,2,0,1:T(1,128)S(1)}, u32[]{:S(2)}, u32[]{:S(2)}) collective-permute-start(f32[3,2,1,128]{3,2,0,1:T(1,128)S(1)} %get-tuple-element.234), channel_id=1, source_target_pairs={{0,8},{8,16},{16,24},{24,0},{1,9},{9,17},{17,25},{25,1},{2,10},{10... | collective-permute-start | bytes 9224 | tf_op jit(solution)/shard_map/ppermute | solution.py:26
  61.7 3.6 %collective-permute-start.9 = (f32[3,2,1,128]{3,2,0,1:T(1,128)S(1)}, f32[3,2,1,128]{3,2,0,1:T(1,128)S(1)}, u32[]{:S(2)}, u32[]{:S(2)}) collective-permute-start(f32[3,2,1,128]{3,2,0,1:T(1,128)S(1)} %get-tuple-element.235), channel_id=1, source_target_pairs={{8,0},{16,8},{24,16},{0,24},{9,1},{17,9},{25,17},{1,25},{10,2},{18... | collective-permute-start | bytes 9224 | tf_op jit(solution)/shard_map/ppermute | solution.py:27
  65.4 5.3 %collective-permute-start.10 = (f32[3,2,10,1]{3,2,0,1:T(8,128)S(1)}, f32[3,2,10,1]{3,2,0,1:T(8,128)S(1)}, u32[]{:S(2)}, u32[]{:S(2)}) collective-permute-start(f32[3,2,10,1]{3,2,0,1:T(8,128)S(1)} %get-tuple-element.227), channel_id=1, source_target_pairs={{0,1},{1,2},{2,3},{3,4},{4,5},{5,6},{6,7},{7,0},{8,9},{9,10},{10,1... | collective-permute-start | bytes 728 | tf_op jit(solution)/shard_map/ppermute | solution.py:26
  65.4 5.3 %collective-permute-start.11 = (f32[3,2,10,1]{3,2,0,1:T(8,128)S(1)}, f32[3,2,10,1]{3,2,0,1:T(8,128)S(1)}, u32[]{:S(2)}, u32[]{:S(2)}) collective-permute-start(f32[3,2,10,1]{3,2,0,1:T(8,128)S(1)} %get-tuple-element.226), channel_id=1, source_target_pairs={{1,0},{2,1},{3,2},{4,3},{5,4},{6,5},{7,6},{0,7},{9,8},{10,9},{11,1... | collective-permute-start | bytes 728 | tf_op jit(solution)/shard_map/ppermute | solution.py:27
where the time goes:
time: 74 us; the launch traced here: 73.5 us
  local copies, waits for them, and re-layouts  23.7 us (32%)
  starting transfers between devices  20.5 us (28%)
  blocking collectives  16.3 us (22%)
  waiting for transfers between devices  5.93 us (8%)
  other arithmetic  5.43 us (7%)
  between operations  1.17 us (2%)
    ppermute x6, starting transfers between devices, with_halo(): after = lax.ppermute(leading, axis, down)  15.2 us
    gather x2, local copies, waits for them, and re-layouts, shards(): jnp.take(wide_stiff, lookup)  12.3 us
    all_gather x1, blocking collectives, shards(): lax.all_gather(facets, 'mesh', axis=0, tiled=True)  8.77 us
    all_gather x1, blocking collectives, shards(): lax.all_gather(penalty, 'mesh', axis=0, tiled=True)  7.49 us
    gather x2, local copies, waits for them, and re-layouts, shards(): facet_rows = jnp.take(wide_table, lookup, axis=1)  5.62 us
    ppermute x6, waiting for transfers between devices, with_halo(): before = lax.ppermute(last, axis, up)  5.58 us
    ppermute x6, starting transfers between devices, with_halo(): before = lax.ppermute(last, axis, up)  5.34 us
    slice x4, local copies, waits for them, and re-layouts, with_halo(): last = lax.slice_in_dim(shard, length - width, length, axis=dim)  1.68 us
  transfers between devices with their start and end apart: 12, of which 5 were waited for; matrix products, arithmetic and copies ran while one was open for 33% of the time, Pallas kernels for 0%

commit v1 on v0

v1 whole, which is shorter than its diff:
```python
import functools

import jax
import jax.numpy as jnp
from jax import lax
from jax.experimental import pallas as pl
from jax.experimental.pallas import tpu as pltpu
from jax.sharding import PartitionSpec as P

TIME_STEP = 0.1
MESH = pl.DeviceIdType.MESH
ROWS = 8
LANES = 128
DIRECTIONS = ((0, 1), (0, -1), (1, 0), (-1, 0), (1, 1), (1, -1), (-1, 1), (-1, -1))
SLOT = {d: i for i, d in enumerate(DIRECTIONS)}
PAD = 24


def kernel(
    n_mesh,
    n_sub,
    steps,
    stiff,
    owners,
    disp_hbm,
    vel_hbm,
    mass_hbm,
    moduli_hbm,
    surf_hbm,
    facets_hbm,
    penalty_hbm,
    pairs_hbm,
    out_disp,
    out_vel,
    own,
    vel,
    mass,
    surf,
    pairs,
    table,
    pen,
    packed,
    arrived,
    wide,
    found,
    local_sem,
    table_send,
    table_recv,
    pen_send,
    pen_recv,
    halo_send,
    halo_recv,
):
    q, s = lax.axis_index("mesh"), lax.axis_index("sub")

    def at(dq, ds):
        return (lax.rem(q + dq + n_mesh, n_mesh), lax.rem(s + ds + n_sub, n_sub))

    copies = [
        pltpu.make_async_copy(src, dst, local_sem.at[i])
        for i, (src, dst) in enumerate(
            (
                (disp_hbm, own.at[pl.ds(0, 48)]),
                (moduli_hbm, own.at[pl.ds(48, 16)]),
                (facets_hbm, table.at[q]),
                (penalty_hbm, pen.at[q]),
                (pairs_hbm, pairs),
                (surf_hbm, surf),
                (vel_hbm, vel),
                (mass_hbm, mass),
            )
        )
    ]
    barrier = pltpu.get_barrier_semaphore()
    partners = [at(*d) for d in DIRECTIONS if d[1] != 0] + [at(d, 0) for d in range(1, n_mesh)]
    for device in partners:
        pl.semaphore_signal(barrier, inc=1, device_id=device, device_id_type=MESH)
    for copy in copies:
        copy.start()

    lane = lax.broadcasted_iota(jnp.int32, (ROWS, LANES), 1)

    def pack(step, planes, count):
        left = jnp.zeros((ROWS, LANES), jnp.float32)
        right = left
        for p in range(count):
            plane = planes[p]
            left = jnp.where(lane == p, pltpu.roll(plane, p, 1) if p else plane, left)
            right = jnp.where(lane == p, pltpu.roll(plane, p + 1, 1), right)
        packed[step, 0] = left
        packed[step, 1] = right
        packed[step, 2] = own[pl.ds(0, 8, stride=8), :]
        packed[step, 3] = own[pl.ds(7, 8, stride=8), :]

    def halo(step):
        made = []
        for i, (dq, ds) in enumerate(DIRECTIONS):
            source = (2 if dq < 0 else 3) if dq else (0 if ds < 0 else 1)
            made.append(
                pltpu.make_async_remote_copy(
                    src_ref=packed.at[step, source],
                    dst_ref=arrived.at[step, i],
                    send_sem=halo_send.at[step, i],
                    recv_sem=halo_recv.at[step, i],
                    device_id=at(dq, ds),
                    device_id_type=MESH,
                )
            )
        return made

    copies[0].wait()
    copies[1].wait()
    pack(0, [own[pl.ds(8 * p, 8), :] for p in range(8)], 8)
    copies[2].wait()
    copies[3].wait()
    pl.semaphore_wait(barrier, len(partners))
    halos = halo(0)
    for copy in halos:
        copy.start()
    shared = []
    for d in range(1, n_mesh):
        for ref, send, recv in ((table, table_send, table_recv), (pen, pen_send, pen_recv)):
            shared.append(
                pltpu.make_async_remote_copy(
                    src_ref=ref.at[q],
                    dst_ref=ref.at[q],
                    send_sem=send.at[d - 1],
                    recv_sem=recv.at[d - 1],
                    device_id=at(d, 0),
                    device_id_type=MESH,
                )
            )
    for copy in shared:
        copy.start()
    for copy in copies[4:]:
        copy.wait()
    inverse = [TIME_STEP / mass[pl.ds(8 * a, 8), :] for a in range(2)]

    def gather(step):
        for b in range(ROWS):
            owner = owners[step, b]
            index = jnp.broadcast_to(pairs[pl.ds(step * ROWS + b, 1), :], (ROWS, LANES))
            chunk, place = index >> 7, index & 127
            total = jnp.zeros((ROWS, LANES), jnp.float32)
            for k in range(table.shape[2] // LANES):
                columns = pl.ds(k * LANES, LANES)
                stiffness_row = pen[owner, :, columns]
                rows = jnp.concatenate([table[owner, :, columns], stiffness_row, stiffness_row], axis=0)
                picked = jnp.take_along_axis(rows, place, axis=1, mode="promise_in_bounds")
                total = jnp.where(chunk == k, picked, total)
            found[step, pl.ds(8 * b, 8), :] = total

    def spread(step, planes, count):
        from_left, from_right = arrived[step, SLOT[(0, 1)]], arrived[step, SLOT[(0, -1)]]
        for p in range(count):
            plane = planes[p]
            before = pltpu.roll(from_left, LANES - p, 1) if p else from_left
            after = pltpu.roll(from_right, LANES - 1 - p, 1)
            rows = pl.ds(p * PAD + 8, 8)
            wide[0, rows, :] = jnp.where(lane == 0, before, pltpu.roll(plane, 1, 1))
            wide[1, rows, :] = plane
            wide[2, rows, :] = jnp.where(lane == LANES - 1, after, pltpu.roll(plane, LANES - 1, 1))
        for dq, row in ((1, 7), (-1, 16)):
            centre = arrived[step, SLOT[(dq, 0)]]
            west, east = arrived[step, SLOT[(dq, 1)]], arrived[step, SLOT[(dq, -1)]]
            rows = pl.ds(row, 8, stride=PAD)
            wide[0, rows, :] = pltpu.roll(jnp.where(lane == LANES - 1, west, centre), 1, 1)
            wide[1, rows, :] = centre
            wide[2, rows, :] = pltpu.roll(jnp.where(lane == 0, east, centre), LANES - 1, 1)

    def shifted(p, di, dj):
        return wide[dj + 1, pl.ds(p * PAD + 8 + di, 8), :]

    scales = {}
    planes = [own[pl.ds(8 * p, 8), :] for p in range(8)]
    for step in range(steps):
        if step == 0:
            for copy in shared:
                copy.wait_recv()
        gather(step)
        for copy in halos:
            copy.wait_recv()
        spread(step, planes, 8 if step == 0 else 6)
        if step == 0:
            both = {
                (di, dj): shifted(6, di, dj) + shifted(7, di, dj) for di in (-1, 0, 1) for dj in (-1, 0, 1)
            }
            for b in (0, 1):
                for e in (0, 1):
                    scales[b, e] = 0.125 * (
                        (both[-b, -e] + both[-b, 1 - e]) + (both[1 - b, -e] + both[1 - b, 1 - e])
                    )
        force = [None] * 6
        for b in (0, 1):
            for e in (0, 1):
                sums = [None] * 6
                for corner in range(8):
                    a2, b2, e2 = corner >> 2, (corner >> 1) & 1, corner & 1
                    for m2 in range(3):
                        value = shifted(2 * m2 + a2, b2 - b, e2 - e)
                        for a in (0, 1):
                            for m in range(3):
                                row = 3 * (4 * a + 2 * b + e) + m
                                term = stiff[row, 3 * corner + m2] * value
                                o = 2 * m + a
                                sums[o] = term if sums[o] is None else sums[o] + term
                for o in range(6):
                    term = scales[b, e] * sums[o]
                    force[o] = term if force[o] is None else force[o] + term
        facet = [found[step, pl.ds(c, 8, stride=8), :] for c in range(7)]
        points = [surf[pl.ds(8 * m, 8), :] + planes[2 * m] for m in range(3)]
        gap = sum(facet[3 + m] * (points[m] - facet[m]) for m in range(3))
        strength = facet[6] * jnp.maximum(-gap, 0.0)
        last = step == steps - 1
        fresh = []
        for o in range(6):
            m, a = o // 2, o % 2
            net = facet[3 + m] * strength - force[o] if a == 0 else -force[o]
            rows = pl.ds(8 * o, 8)
            speed = vel[rows, :] + inverse[a] * net
            moved = planes[o] + TIME_STEP * speed
            fresh.append(moved)
            if last:
                out_vel[rows, :] = speed
                out_disp[rows, :] = moved
            else:
                vel[rows, :] = speed
                own[rows, :] = moved
        for copy in halos:
            copy.wait_send()
        planes = fresh
        if not last:
            pack(step + 1, planes, 6)
            halos = halo(step + 1)
            for copy in halos:
                copy.start()
    for copy in shared:
        copy.wait_send()


def shards(
    displacement,
    velocity,
    node_mass,
    moduli,
    stiffness,
    surface_ref,
    facets,
    penalty,
    owners,
    facet_pairs,
):
    steps = owners.shape[0]
    width = facets.shape[3]
    n_mesh, n_sub = lax.axis_size("mesh"), lax.axis_size("sub")
    assert displacement.shape == (3, 2, ROWS, LANES)
    f32 = jnp.float32
    out = jax.ShapeDtypeStruct((6 * ROWS, LANES), f32)
    smem = pl.BlockSpec(memory_space=pltpu.SMEM)
    anywhere = pl.BlockSpec(memory_space=pl.ANY)
    vmem = pl.BlockSpec(memory_space=pltpu.VMEM)
    dma = pltpu.SemaphoreType.DMA
    moved, speed = pl.pallas_call(
        functools.partial(kernel, n_mesh, n_sub, steps),
        out_shape=(out, out),
        in_specs=[smem, smem] + [anywhere] * 8,
        out_specs=(vmem, vmem),
        scratch_shapes=[
            pltpu.VMEM((8 * ROWS, LANES), f32),
            pltpu.VMEM((6 * ROWS, LANES), f32),
            pltpu.VMEM((2 * ROWS, LANES), f32),
            pltpu.VMEM((3 * ROWS, LANES), f32),
            pltpu.VMEM((steps * ROWS, LANES), jnp.int32),
            pltpu.VMEM((n_mesh, 6, width), f32),
            pltpu.VMEM((n_mesh, 1, width), f32),
            pltpu.VMEM((steps, 4, ROWS, LANES), f32),
            pltpu.VMEM((steps, 8, ROWS, LANES), f32),
            pltpu.VMEM((3, 8 * PAD, LANES), f32),
            pltpu.VMEM((steps, 8 * ROWS, LANES), f32),
            dma((8,)),
            dma((n_mesh - 1,)),
            dma((n_mesh - 1,)),
            dma((n_mesh - 1,)),
            dma((n_mesh - 1,)),
            dma((steps, 8)),
            dma((steps, 8)),
        ],
        compiler_params=pltpu.CompilerParams(collective_id=0, has_side_effects=True),
    )(
        stiffness,
        owners.reshape(steps, ROWS),
        displacement.reshape(6 * ROWS, LANES),
        velocity.reshape(6 * ROWS, LANES),
        node_mass.reshape(2 * ROWS, LANES),
        moduli.reshape(2 * ROWS, LANES),
        surface_ref.reshape(3 * ROWS, LANES),
        facets.reshape(6, width),
        penalty.reshape(1, width),
        facet_pairs.reshape(steps * ROWS, LANES),
    )
    return moved.reshape(displacement.shape), speed.reshape(velocity.shape)


def solution(mesh):
    in_specs = (
        P(None, None, "mesh", "sub"),
        P(None, None, "mesh", "sub"),
        P(None, "mesh", "sub"),
        P(None, "mesh", "sub"),
        P(),
        P(None, "mesh", "sub"),
        P("mesh", "sub", None, None),
        P("mesh", "sub", None),
        P(None, "mesh", "sub", None, None),
        P(None, "mesh", "sub"),
    )
    out_specs = (P(None, None, "mesh", "sub"), P(None, None, "mesh", "sub"))
    return jax.shard_map(shards, mesh=mesh, in_specs=in_specs, out_specs=out_specs, check_vma=False)
```

time: 74 us -> 21.5 us (0.29)
  starting transfers between devices: 20.5 us -> 0 us
  local copies, waits for them, and re-layouts: 23.7 us -> 3.31 us
  Pallas kernels: 0 us -> 17.2 us
  blocking collectives: 16.3 us -> 0 us
  waiting for transfers between devices: 5.93 us -> 0 us
  other arithmetic: 5.43 us -> 0 us
    ppermute x12 -> x0, starting transfers between devices: 20.5 us -> none  [the longest x6 15.2 us: with_halo(): after = lax.ppermute(leading, axis, down)]
    gather x4 -> x0, local copies, waits for them, and re-layouts: 17.9 us -> none  [the longest x2 12.3 us: shards(): jnp.take(wide_stiff, lookup)]
    pallas_call x0 -> x1, Pallas kernels: none -> 17.2 us  [shards(): pl.pallas_call(functools.partial(kernel, n_mesh, n_sub, steps), out_shape...]
    all_gather x2 -> x0, blocking collectives: 16.3 us -> none  [the longest x1 8.77 us: shards(): lax.all_gather(facets, 'mesh', axis=0, tiled=True)]
    ppermute x12 -> x0, waiting for transfers between devices: 5.93 us -> none  [the longest x6 5.58 us: with_halo(): before = lax.ppermute(last, axis, up)]
    slice x8 -> x0, local copies, waits for them, and re-layouts: 1.98 us -> none  [the longest x4 1.68 us: with_halo(): last = lax.slice_in_dim(shard, length - width, length, axis=dim)]
    unnamed x30 -> x5, local copies, waits for them, and re-layouts: 1.36 us -> 3.31 us
    mul x8 -> x0, other arithmetic: 1.42 us -> none  [the longest x1 0.67 us: shards(): lookup = (destination[:, None] * table_width + pair_rows).reshape(-1)]
  transfers between devices with their start and end apart: 12 -> 0, of which waited for: 5 -> 0; matrix products, arithmetic and copies ran while one was open for 33% -> 0% of each run, Pallas kernels for 0% -> 0%
where the time goes in v1:
time: 21.5 us; the launch traced here: 21.2 us
  Pallas kernels  17.2 us (80%)
  local copies, waits for them, and re-layouts  3.31 us (15%)
  between operations  0.65 us (3%)
    pallas_call x1, Pallas kernels, shards(): pl.pallas_call(functools.partial(kernel, n_mesh, n_sub, steps), out_shape...  17.2 us
    unnamed x5, local copies, waits for them, and re-layouts  3.31 us

profile of v1, /device:TPU:0, one launch (start us, length us, event | category | flops | bytes accessed | tf_op | source)
XLA Modules:
  0.0 21.2 jit_solution(6382785441068267709)
XLA Ops:
  0.6 1.3 %copy.14 = f32[1,1,6,1024]{3,2,1,0:T(8,128)} copy(f32[1,1,6,1024]{3,1,2,0:T(1,128)} %param.16) | data formatting | bytes 49152
  2.0 17.2 %shard_map.113 = (f32[48,128]{1,0:T(8,128)}, f32[48,128]{1,0:T(8,128)}) custom-call(f32[24,24]{1,0:T(8,128)} %stiff.1, s32[2,8]{1,0:T(2,128)} %bitcast.23, f32[48,128]{1,0:T(8,128)} %bitcast.16, f32[48,128]{1,0:T(8,128)} %bitcast.17, f32[16,128]{1,0:T(8,128)} %bitcast.19, f32[16,128]{1,0:T(8,128)} %bitcast.20, f32[24,128]{1,0:T(8,128)} %bitcast.18, ...), custom_call_target="tpu_custom_call" | custom-call | tf_op jit(solution)/shard_map/pallas_call | solution.py:263
  19.2 0.0 copy-start
  19.2 1.4 %copy.17 = f32[3,2,8,128]{3,2,1,0:T(8,128)} copy(f32[3,2,8,128]{3,2,1,0:T(8,128)} %bitcast.15) | data formatting | bytes 49152
  20.6 0.0 copy-done
  20.6 0.6 %copy.18 = f32[3,2,8,128]{3,2,1,0:T(8,128)} copy(f32[3,2,8,128]{3,2,1,0:T(8,128)S(1)} %bitcast.14) | data formatting | bytes 49152
Async XLA Ops:
  19.2 1.4 %copy-start = (f32[48,128]{1,0:T(8,128)S(1)}, f32[48,128]{1,0:T(8,128)}, u32[]{:S(2)}) copy-start(f32[48,128]{1,0:T(8,128)} %get-tuple-element.5) | copy-start | bytes 73732

commit v2 on v1

--- a/solution.py
+++ b/solution.py
@@ -20,8 +20,8 @@
     n_mesh,
     n_sub,
     steps,
-    stiff,
-    owners,
+    stiff_hbm,
+    owners_hbm,
     disp_hbm,
     vel_hbm,
     mass_hbm,
@@ -32,13 +32,14 @@
     pairs_hbm,
     out_disp,
     out_vel,
+    stiff,
+    owners,
     own,
     vel,
     mass,
     surf,
     pairs,
     table,
-    pen,
     packed,
     arrived,
     wide,
@@ -46,8 +47,6 @@
     local_sem,
     table_send,
     table_recv,
-    pen_send,
-    pen_recv,
     halo_send,
     halo_recv,
 ):
@@ -56,18 +55,21 @@
     def at(dq, ds):
         return (lax.rem(q + dq + n_mesh, n_mesh), lax.rem(s + ds + n_sub, n_sub))
 
+    chunks = table.shape[1] // 8
     copies = [
         pltpu.make_async_copy(src, dst, local_sem.at[i])
         for i, (src, dst) in enumerate(
             (
                 (disp_hbm, own.at[pl.ds(0, 48)]),
                 (moduli_hbm, own.at[pl.ds(48, 16)]),
-                (facets_hbm, table.at[q]),
-                (penalty_hbm, pen.at[q]),
+                (facets_hbm, table.at[q, pl.ds(0, 6 * chunks)]),
+                (penalty_hbm, table.at[q, pl.ds(6 * chunks, chunks)]),
                 (pairs_hbm, pairs),
                 (surf_hbm, surf),
                 (vel_hbm, vel),
                 (mass_hbm, mass),
+                (stiff_hbm, stiff),
+                (owners_hbm, owners),
             )
         )
     ]
@@ -108,6 +110,8 @@
             )
         return made
 
+    for o in range(n_mesh):
+        table[o, pl.ds(7 * chunks, chunks), :] = jnp.zeros((chunks, LANES), jnp.float32)
     copies[0].wait()
     copies[1].wait()
     pack(0, [own[pl.ds(8 * p, 8), :] for p in range(8)], 8)
@@ -119,17 +123,17 @@
         copy.start()
     shared = []
     for d in range(1, n_mesh):
-        for ref, send, recv in ((table, table_send, table_recv), (pen, pen_send, pen_recv)):
-            shared.append(
-                pltpu.make_async_remote_copy(
-                    src_ref=ref.at[q],
-                    dst_ref=ref.at[q],
-                    send_sem=send.at[d - 1],
-                    recv_sem=recv.at[d - 1],
-                    device_id=at(d, 0),
-                    device_id_type=MESH,
-                )
+        used = table.at[q, pl.ds(0, 7 * chunks)]
+        shared.append(
+            pltpu.make_async_remote_copy(
+                src_ref=used,
+                dst_ref=used,
+                send_sem=table_send.at[d - 1],
+                recv_sem=table_recv.at[d - 1],
+                device_id=at(d, 0),
+                device_id_type=MESH,
             )
+        )
     for copy in shared:
         copy.start()
     for copy in copies[4:]:
@@ -142,10 +146,8 @@
             index = jnp.broadcast_to(pairs[pl.ds(step * ROWS + b, 1), :], (ROWS, LANES))
             chunk, place = index >> 7, index & 127
             total = jnp.zeros((ROWS, LANES), jnp.float32)
-            for k in range(table.shape[2] // LANES):
-                columns = pl.ds(k * LANES, LANES)
-                stiffness_row = pen[owner, :, columns]
-                rows = jnp.concatenate([table[owner, :, columns], stiffness_row, stiffness_row], axis=0)
+            for k in range(chunks):
+                rows = table[owner, pl.ds(k, 8, stride=chunks), :]
                 picked = jnp.take_along_axis(rows, place, axis=1, mode="promise_in_bounds")
                 total = jnp.where(chunk == k, picked, total)
             found[step, pl.ds(8 * b, 8), :] = total
@@ -255,31 +257,29 @@
     n_mesh, n_sub = lax.axis_size("mesh"), lax.axis_size("sub")
     assert displacement.shape == (3, 2, ROWS, LANES)
     f32 = jnp.float32
-    out = jax.ShapeDtypeStruct((6 * ROWS, LANES), f32)
-    smem = pl.BlockSpec(memory_space=pltpu.SMEM)
+    out = pltpu.VMEM((6 * ROWS, LANES), f32)
     anywhere = pl.BlockSpec(memory_space=pl.ANY)
     vmem = pl.BlockSpec(memory_space=pltpu.VMEM)
     dma = pltpu.SemaphoreType.DMA
     moved, speed = pl.pallas_call(
         functools.partial(kernel, n_mesh, n_sub, steps),
         out_shape=(out, out),
-        in_specs=[smem, smem] + [anywhere] * 8,
+        in_specs=[anywhere] * 10,
         out_specs=(vmem, vmem),
         scratch_shapes=[
+            pltpu.SMEM((24, 24), f32),
+            pltpu.SMEM((steps, ROWS), jnp.int32),
             pltpu.VMEM((8 * ROWS, LANES), f32),
             pltpu.VMEM((6 * ROWS, LANES), f32),
             pltpu.VMEM((2 * ROWS, LANES), f32),
             pltpu.VMEM((3 * ROWS, LANES), f32),
             pltpu.VMEM((steps * ROWS, LANES), jnp.int32),
-            pltpu.VMEM((n_mesh, 6, width), f32),
-            pltpu.VMEM((n_mesh, 1, width), f32),
+            pltpu.VMEM((n_mesh, 8 * width // LANES, LANES), f32),
             pltpu.VMEM((steps, 4, ROWS, LANES), f32),
             pltpu.VMEM((steps, 8, ROWS, LANES), f32),
             pltpu.VMEM((3, 8 * PAD, LANES), f32),
             pltpu.VMEM((steps, 8 * ROWS, LANES), f32),
-            dma((8,)),
-            dma((n_mesh - 1,)),
-            dma((n_mesh - 1,)),
+            dma((10,)),
             dma((n_mesh - 1,)),
             dma((n_mesh - 1,)),
             dma((steps, 8)),
@@ -294,8 +294,8 @@
         node_mass.reshape(2 * ROWS, LANES),
         moduli.reshape(2 * ROWS, LANES),
         surface_ref.reshape(3 * ROWS, LANES),
-        facets.reshape(6, width),
-        penalty.reshape(1, width),
+        facets.transpose(0, 2, 1, 3).reshape(6 * width // LANES, LANES),
+        penalty.reshape(width // LANES, LANES),
         facet_pairs.reshape(steps * ROWS, LANES),
     )
     return moved.reshape(displacement.shape), speed.reshape(velocity.shape)

time: 21.5 us -> 17.7 us (0.82)
  local copies, waits for them, and re-layouts: 3.31 us -> 1.22 us
  Pallas kernels: 17.2 us -> 15.6 us
    unnamed x5 -> x2, local copies, waits for them, and re-layouts: 3.31 us -> 1.22 us
    pallas_call x1, Pallas kernels: 17.2 us -> 15.6 us  [shards(): pl.pallas_call(functools.partial(kernel, n_mesh, n_sub, steps), out_shape...]
where the time goes in v2:
time: 17.7 us; the launch traced here: 17.5 us
  Pallas kernels  15.6 us (88%)
  local copies, waits for them, and re-layouts  1.22 us (7%)
  between operations  0.64 us (4%)
    pallas_call x1, Pallas kernels, shards(): pl.pallas_call(functools.partial(kernel, n_mesh, n_sub, steps), out_shape...  15.6 us
    unnamed x2, local copies, waits for them, and re-layouts  1.22 us

profile of v2, /device:TPU:0, one launch (start us, length us, event | category | flops | bytes accessed | tf_op | source)
XLA Modules:
  0.0 17.5 jit_solution(9055549035319027440)
XLA Ops:
  0.6 15.6 %shard_map.113 = (f32[48,128]{1,0:T(8,128)S(1)}, f32[48,128]{1,0:T(8,128)S(1)}) custom-call(f32[24,24]{1,0:T(8,128)} %stiff_hbm.1, s32[2,8]{1,0:T(2,128)} %bitcast.21, f32[48,128]{1,0:T(8,128)} %bitcast.13, f32[48,128]{1,0:T(8,128)} %bitcast.14, f32[16,128]{1,0:T(8,128)} %bitcast.17, f32[16,128]{1,0:T(8,128)} %bitcast.18, f32[24,128]{1,0:T(8,128)} %bitcast.16, ...), custom_call_target="tpu_custom_call" | custom-call | tf_op jit(solution)/shard_map/pallas_call | solution.py:264
  16.3 0.6 %copy.14 = f32[3,2,8,128]{3,2,1,0:T(8,128)} copy(f32[3,2,8,128]{3,2,1,0:T(8,128)S(1)} %bitcast.12) | data formatting | bytes 49152
  16.9 0.6 %copy.15 = f32[3,2,8,128]{3,2,1,0:T(8,128)} copy(f32[3,2,8,128]{3,2,1,0:T(8,128)S(1)} %bitcast.11) | data formatting | bytes 49152

commit v3 on v2

--- a/solution.py
+++ b/solution.py
@@ -11,7 +11,7 @@
 MESH = pl.DeviceIdType.MESH
 ROWS = 8
 LANES = 128
-DIRECTIONS = ((0, 1), (0, -1), (1, 0), (-1, 0), (1, 1), (1, -1), (-1, 1), (-1, -1))
+DIRECTIONS = ((1, 1), (1, -1), (-1, 1), (-1, -1), (1, 0), (-1, 0), (0, 1), (0, -1))
 SLOT = {d: i for i, d in enumerate(DIRECTIONS)}
 PAD = 24
 
@@ -91,6 +91,8 @@
             right = jnp.where(lane == p, pltpu.roll(plane, p + 1, 1), right)
         packed[step, 0] = left
         packed[step, 1] = right
+
+    def pack_rows(step):
         packed[step, 2] = own[pl.ds(0, 8, stride=8), :]
         packed[step, 3] = own[pl.ds(7, 8, stride=8), :]
 
@@ -114,6 +116,7 @@
         table[o, pl.ds(7 * chunks, chunks), :] = jnp.zeros((chunks, LANES), jnp.float32)
     copies[0].wait()
     copies[1].wait()
+    pack_rows(0)
     pack(0, [own[pl.ds(8 * p, 8), :] for p in range(8)], 8)
     copies[2].wait()
     copies[3].wait()
@@ -152,22 +155,25 @@
                 total = jnp.where(chunk == k, picked, total)
             found[step, pl.ds(8 * b, 8), :] = total
 
-    def spread(step, planes, count):
+    def spread_middle(step, planes, count):
+        for p in range(count):
+            wide[1, pl.ds(p * PAD + 8, 8), :] = planes[p]
+        for dq, row in ((1, 7), (-1, 16)):
+            wide[1, pl.ds(row, 8, stride=PAD), :] = arrived[step, SLOT[(dq, 0)]]
+
+    def spread_sides(step, turned, count):
         from_left, from_right = arrived[step, SLOT[(0, 1)]], arrived[step, SLOT[(0, -1)]]
         for p in range(count):
-            plane = planes[p]
             before = pltpu.roll(from_left, LANES - p, 1) if p else from_left
             after = pltpu.roll(from_right, LANES - 1 - p, 1)
             rows = pl.ds(p * PAD + 8, 8)
-            wide[0, rows, :] = jnp.where(lane == 0, before, pltpu.roll(plane, 1, 1))
-            wide[1, rows, :] = plane
-            wide[2, rows, :] = jnp.where(lane == LANES - 1, after, pltpu.roll(plane, LANES - 1, 1))
+            wide[0, rows, :] = jnp.where(lane == 0, before, turned[p][0])
+            wide[2, rows, :] = jnp.where(lane == LANES - 1, after, turned[p][1])
         for dq, row in ((1, 7), (-1, 16)):
             centre = arrived[step, SLOT[(dq, 0)]]
             west, east = arrived[step, SLOT[(dq, 1)]], arrived[step, SLOT[(dq, -1)]]
             rows = pl.ds(row, 8, stride=PAD)
             wide[0, rows, :] = pltpu.roll(jnp.where(lane == LANES - 1, west, centre), 1, 1)
-            wide[1, rows, :] = centre
             wide[2, rows, :] = pltpu.roll(jnp.where(lane == 0, east, centre), LANES - 1, 1)
 
     def shifted(p, di, dj):
@@ -180,9 +186,37 @@
             for copy in shared:
                 copy.wait_recv()
         gather(step)
-        for copy in halos:
-            copy.wait_recv()
-        spread(step, planes, 8 if step == 0 else 6)
+        facet = [found[step, pl.ds(c, 8, stride=8), :] for c in range(7)]
+        points = [surf[pl.ds(8 * m, 8), :] + planes[2 * m] for m in range(3)]
+        gap = sum(facet[3 + m] * (points[m] - facet[m]) for m in range(3))
+        strength = facet[6] * jnp.maximum(-gap, 0.0)
+        push = [facet[3 + m] * strength for m in range(3)]
+        count = 8 if step == 0 else 6
+        turned = [(pltpu.roll(p, 1, 1), pltpu.roll(p, LANES - 1, 1)) for p in planes[:count]]
+        sums = {(b, e): [None] * 6 for b in (0, 1) for e in (0, 1)}
+
+        def accumulate(middle):
+            for b, e in sums:
+                for corner in range(8):
+                    a2, b2, e2 = corner >> 2, (corner >> 1) & 1, corner & 1
+                    if (e2 == e) != middle:
+                        continue
+                    for m2 in range(3):
+                        value = shifted(2 * m2 + a2, b2 - b, e2 - e)
+                        for o in range(6):
+                            row = 3 * (4 * (o % 2) + 2 * b + e) + o // 2
+                            term = stiff[row, 3 * corner + m2] * value
+                            before = sums[b, e][o]
+                            sums[b, e][o] = term if before is None else before + term
+
+        for d in ((1, 0), (-1, 0)):
+            halos[SLOT[d]].wait_recv()
+        spread_middle(step, planes, count)
+        accumulate(True)
+        for d in DIRECTIONS:
+            if d[1] != 0:
+                halos[SLOT[d]].wait_recv()
+        spread_sides(step, turned, count)
         if step == 0:
             both = {
                 (di, dj): shifted(6, di, dj) + shifted(7, di, dj) for di in (-1, 0, 1) for dj in (-1, 0, 1)
@@ -192,32 +226,17 @@
                     scales[b, e] = 0.125 * (
                         (both[-b, -e] + both[-b, 1 - e]) + (both[1 - b, -e] + both[1 - b, 1 - e])
                     )
+        accumulate(False)
         force = [None] * 6
-        for b in (0, 1):
-            for e in (0, 1):
-                sums = [None] * 6
-                for corner in range(8):
-                    a2, b2, e2 = corner >> 2, (corner >> 1) & 1, corner & 1
-                    for m2 in range(3):
-                        value = shifted(2 * m2 + a2, b2 - b, e2 - e)
-                        for a in (0, 1):
-                            for m in range(3):
-                                row = 3 * (4 * a + 2 * b + e) + m
-                                term = stiff[row, 3 * corner + m2] * value
-                                o = 2 * m + a
-                                sums[o] = term if sums[o] is None else sums[o] + term
-                for o in range(6):
-                    term = scales[b, e] * sums[o]
-                    force[o] = term if force[o] is None else force[o] + term
-        facet = [found[step, pl.ds(c, 8, stride=8), :] for c in range(7)]
-        points = [surf[pl.ds(8 * m, 8), :] + planes[2 * m] for m in range(3)]
-        gap = sum(facet[3 + m] * (points[m] - facet[m]) for m in range(3))
-        strength = facet[6] * jnp.maximum(-gap, 0.0)
+        for b, e in sums:
+            for o in range(6):
+                term = scales[b, e] * sums[b, e][o]
+                force[o] = term if force[o] is None else force[o] + term
         last = step == steps - 1
         fresh = []
         for o in range(6):
             m, a = o // 2, o % 2
-            net = facet[3 + m] * strength - force[o] if a == 0 else -force[o]
+            net = push[m] - force[o] if a == 0 else -force[o]
             rows = pl.ds(8 * o, 8)
             speed = vel[rows, :] + inverse[a] * net
             moved = planes[o] + TIME_STEP * speed
@@ -228,16 +247,33 @@
             else:
                 vel[rows, :] = speed
                 own[rows, :] = moved
-        for copy in halos:
+        planes = fresh
+        sent = halos
+        if not last:
+            halos = halo(step + 1)
+            pack_rows(step + 1)
+            for d in DIRECTIONS:
+                if d[0] != 0:
+                    halos[SLOT[d]].start()
+            pack(step + 1, planes, 6)
+            for d in DIRECTIONS:
+                if d[0] == 0:
+                    halos[SLOT[d]].start()
+        for copy in sent:
             copy.wait_send()
-        planes = fresh
-        if not last:
-            pack(step + 1, planes, 6)
-            halos = halo(step + 1)
-            for copy in halos:
-                copy.start()
     for copy in shared:
         copy.wait_send()
+
+
+def flush(moved, speed, out_moved, out_speed, sem):
+    copies = [
+        pltpu.make_async_copy(src, dst, sem.at[i])
+        for i, (src, dst) in enumerate(((moved, out_moved), (speed, out_speed)))
+    ]
+    for copy in copies:
+        copy.start()
+    for copy in copies:
+        copy.wait()
 
 
 def shards(
@@ -298,6 +334,14 @@
         penalty.reshape(width // LANES, LANES),
         facet_pairs.reshape(steps * ROWS, LANES),
     )
+    moved, speed = pl.pallas_call(
+        flush,
+        out_shape=[jax.ShapeDtypeStruct((6 * ROWS, LANES), f32)] * 2,
+        in_specs=[anywhere, anywhere],
+        out_specs=[anywhere, anywhere],
+        scratch_shapes=[dma((2,))],
+        compiler_params=pltpu.CompilerParams(vmem_limit_bytes=1 << 20),
+    )(pltpu.with_memory_space_constraint(moved, pltpu.VMEM), pltpu.with_memory_space_constraint(speed, pltpu.VMEM))
     return moved.reshape(displacement.shape), speed.reshape(velocity.shape)
 
 

time: 17.7 us -> 16.7 us (0.944)
  local copies, waits for them, and re-layouts: 1.22 us -> 0 us
  Pallas kernels: 15.6 us -> 15.9 us
    unnamed x2 -> x0, local copies, waits for them, and re-layouts: 1.22 us -> none
    pallas_call x0 -> x1, Pallas kernels: none -> 0.64 us  [shards(): pl.pallas_call(flush, out_shape=[jax.ShapeDtypeStruct((6 * ROWS, LANES),...]
    pallas_call x1, Pallas kernels: 15.6 us -> 15.3 us  [shards(): pl.pallas_call(functools.partial(kernel, n_mesh, n_sub, steps), out_shape...]
where the time goes in v3:
time: 16.7 us; the launch traced here: 16.5 us
  Pallas kernels  15.9 us (95%)
  between operations  0.64 us (4%)
    pallas_call x1, Pallas kernels, shards(): pl.pallas_call(functools.partial(kernel, n_mesh, n_sub, steps), out_shape...  15.3 us
    pallas_call x1, Pallas kernels, shards(): pl.pallas_call(flush, out_shape=[jax.ShapeDtypeStruct((6 * ROWS, LANES),...  0.64 us

profile of v3, /device:TPU:0, one launch (start us, length us, event | category | flops | bytes accessed | tf_op | source)
XLA Modules:
  0.0 16.5 jit_solution(6755367796567733663)
XLA Ops:
  0.6 15.3 %shard_map.113 = (f32[48,128]{1,0:T(8,128)S(1)}, f32[48,128]{1,0:T(8,128)S(1)}) custom-call(f32[24,24]{1,0:T(8,128)} %stiff_hbm.1, s32[2,8]{1,0:T(2,128)} %bitcast.19, f32[48,128]{1,0:T(8,128)} %bitcast.11, f32[48,128]{1,0:T(8,128)} %bitcast.12, f32[16,128]{1,0:T(8,128)} %bitcast.15, f32[16,128]{1,0:T(8,128)} %bitcast.16, f32[24,128]{1,0:T(8,128)} %bitcast.14, ...), custom_call_target="tpu_custom_call" | custom-call | tf_op jit(solution)/shard_map/pallas_call | solution.py:300
  15.9 0.6 %shard_map.114 = (f32[48,128]{1,0:T(8,128)}, f32[48,128]{1,0:T(8,128)}) custom-call(f32[48,128]{1,0:T(8,128)S(1)} %get-tuple-element.6.moved, f32[48,128]{1,0:T(8,128)S(1)} %get-tuple-element.7.speed), custom_call_target="tpu_custom_call" | custom-call | tf_op jit(solution)/shard_map/pallas_call | solution.py:337

commit v4 on v3

--- a/solution.py
+++ b/solution.py
@@ -118,12 +118,12 @@
     copies[1].wait()
     pack_rows(0)
     pack(0, [own[pl.ds(8 * p, 8), :] for p in range(8)], 8)
-    copies[2].wait()
-    copies[3].wait()
     pl.semaphore_wait(barrier, len(partners))
     halos = halo(0)
     for copy in halos:
         copy.start()
+    copies[2].wait()
+    copies[3].wait()
     shared = []
     for d in range(1, n_mesh):
         used = table.at[q, pl.ds(0, 7 * chunks)]

time: 16.7 us -> 16.7 us (level)
  no operation moved by 1% of the time
where the time goes in v4:
time: 16.7 us; the launch traced here: 16.5 us
  Pallas kernels  15.9 us (95%)
  between operations  0.64 us (4%)
    pallas_call x1, Pallas kernels, shards(): pl.pallas_call(functools.partial(kernel, n_mesh, n_sub, steps), out_shape...  15.3 us
    pallas_call x1, Pallas kernels, shards(): pl.pallas_call(flush, out_shape=[jax.ShapeDtypeStruct((6 * ROWS, LANES),...  0.64 us

profile of v4, /device:TPU:0, one launch (start us, length us, event | category | flops | bytes accessed | tf_op | source)
XLA Modules:
  0.0 16.5 jit_solution(5346885881499778514)
XLA Ops:
  0.6 15.3 %shard_map.113 = (f32[48,128]{1,0:T(8,128)S(1)}, f32[48,128]{1,0:T(8,128)S(1)}) custom-call(f32[24,24]{1,0:T(8,128)} %stiff_hbm.1, s32[2,8]{1,0:T(2,128)} %bitcast.19, f32[48,128]{1,0:T(8,128)} %bitcast.11, f32[48,128]{1,0:T(8,128)} %bitcast.12, f32[16,128]{1,0:T(8,128)} %bitcast.15, f32[16,128]{1,0:T(8,128)} %bitcast.16, f32[24,128]{1,0:T(8,128)} %bitcast.14, ...), custom_call_target="tpu_custom_call" | custom-call | tf_op jit(solution)/shard_map/pallas_call | solution.py:300
  15.9 0.6 %shard_map.114 = (f32[48,128]{1,0:T(8,128)}, f32[48,128]{1,0:T(8,128)}) custom-call(f32[48,128]{1,0:T(8,128)S(1)} %get-tuple-element.6.moved, f32[48,128]{1,0:T(8,128)S(1)} %get-tuple-element.7.speed), custom_call_target="tpu_custom_call" | custom-call | tf_op jit(solution)/shard_map/pallas_call | solution.py:337
